TPU v7x, 256 devices: a whole 4x4x8 slice. The times are simulated.
256 devices in a mesh: dp: 16 (over z_lo, x, core), tensor: 16 (over z_hi, y).
Axes of the slice: x: 4, y: 4, z: 8 (z_hi: 4, z_lo: 2; z = z_hi * 2 + z_lo), core: 2. Of those that a mesh axis runs over, the one named last changes fastest.
Arguments:
- activations: bfloat16 [4096, 5120], P('dp'), may hold values from -6 to 6
- grad_out: bfloat16 [4096, 5120], P('dp'), may hold values from -6 to 6
- gate_pre: bfloat16 [4096, 7168], P('dp', 'tensor'), may hold values from -8 to 8
- up_pre: bfloat16 [4096, 7168], P('dp', 'tensor'), may hold values from -6 to 6
- gate_up: bfloat16 [5120, 2, 7168], P('dp', None, 'tensor'), may hold values from -0.078125 to 0.078125
- down_weight: bfloat16 [5120, 7168], P('dp', 'tensor'), may hold values from -0.0625 to 0.0625
Outputs:
- grad_input: bfloat16 [4096, 5120], P('dp')
- grad_gate_up: float32 [5120, 2, 7168], P('dp', None, 'tensor')
- grad_down: float32 [5120, 7168], P('dp', 'tensor')
All inputs are finite; a program needn't handle non-finite values.
Results may differ from a plain program's by a relative error of at most 0.017.
Values may be sent and summed in bfloat16 or wider, within the bound.
No kernel may reach another device: no remote copies, remote signals or barrier semaphores. Data moves between devices by JAX's collectives and lax.ppermute only.
A program may use at most 128 MiB of HBM per device.

v0:
```python
import jax
import jax.numpy as jnp
from jax import lax
from jax.sharding import Mesh
from jax.sharding import PartitionSpec as P

DP = ("dp_0", "dp_1", "dp_2")
TENSOR = ("tensor_0", "tensor_1")


def sum_in_order(pieces, axes, order):
    dims = [lax.axis_size(a) for a in axes]
    pieces = pieces.reshape(*dims, *pieces.shape[1:])
    pieces = pieces.transpose(*order, *range(len(axes), pieces.ndim))
    pieces = pieces.reshape(-1, *pieces.shape[len(axes) :])
    for k in order:
        pieces = lax.psum_scatter(pieces, axes[k], scatter_dimension=0, tiled=True)
    return pieces[0]


def split_up(x, dim, devices):
    dims = x.shape
    pieces = x.reshape(*dims[:dim], devices, dims[dim] // devices, *dims[dim + 1 :])
    return jnp.moveaxis(pieces, dim, 0)


def sum_by_axis(x, axes, order, dim):
    devices = lax.axis_size(axes)
    return sum_in_order(split_up(x, dim, devices), axes, order)


def sum_at_owner(x, axis, dim):
    devices = lax.axis_size(axis)
    pieces = lax.all_to_all(split_up(x, dim, devices), axis, 0, 0, tiled=True)
    return jnp.sum(pieces.astype(jnp.float32), axis=0)


def sum_in_two_steps(x, axes, dim):
    far, near = axes
    own = sum_at_owner(split_up(x, dim, lax.axis_size(far)), near, dim + 1)
    return jnp.sum(
        lax.all_to_all(own.astype(jnp.bfloat16), far, 0, 0, tiled=True).astype(jnp.float32), axis=0
    )


def per_device(activations, grad_out, gate_pre, up_pre, gate_up, down_weight):
    tokens = activations.shape[0]
    hidden_width = down_weight.shape[1]
    dp_count = lax.axis_size(DP)
    slab_rows = down_weight.shape[0]
    gate_wide = gate_pre.astype(jnp.float32)
    up_wide = up_pre.astype(jnp.float32)
    gate_sigmoid = jax.nn.sigmoid(gate_wide)
    gate_silu = gate_wide * gate_sigmoid
    hidden = (gate_silu * up_wide).astype(jnp.bfloat16)
    grad_h = jnp.dot(
        grad_out,
        lax.all_gather(down_weight, DP, axis=0, tiled=True),
        preferred_element_type=jnp.float32,
    )
    grad_gate = grad_h * up_wide * gate_sigmoid * (1.0 + gate_wide * (1.0 - gate_sigmoid))
    grad_up = grad_h * gate_silu
    grad_hidden = (
        jnp.stack([grad_gate, grad_up], axis=1)
        .astype(jnp.bfloat16)
        .reshape(tokens, 2 * hidden_width)
    )
    pieces = lax.all_gather(gate_up, DP, axis=0, tiled=True)
    flattened = pieces.reshape(pieces.shape[0], 2 * hidden_width)
    partial_sum = lax.dot_general(
        grad_hidden, flattened, (((1,), (1,)), ((), ())), preferred_element_type=jnp.float32
    )
    share_block = sum_by_axis(partial_sum.astype(jnp.bfloat16), TENSOR, (1, 0), 0).astype(
        jnp.float32
    )
    grad_input = lax.all_gather(share_block.astype(jnp.bfloat16), TENSOR, axis=0, tiled=True)
    gate_part = lax.dot_general(
        activations, grad_hidden, (((0,), (0,)), ((), ())), preferred_element_type=jnp.float32
    )
    down_part = lax.dot_general(
        grad_out, hidden, (((0,), (0,)), ((), ())), preferred_element_type=jnp.float32
    )
    summed = sum_in_two_steps(
        jnp.concatenate([gate_part, down_part], axis=1).astype(jnp.bfloat16),
        (("dp_0", "dp_1"), "dp_2"),
        0,
    )
    summed = summed / dp_count
    grad_gate_up = summed[:, : 2 * hidden_width].reshape(slab_rows, 2, hidden_width)
    grad_down = summed[:, 2 * hidden_width :]
    return (grad_input, grad_gate_up, grad_down)


def solution(mesh):
    split = Mesh(
        mesh.devices.reshape(2, 4, 2, 4, 4), ("dp_0", "dp_1", "dp_2", "tensor_0", "tensor_1")
    )
    return jax.shard_map(
        per_device,
        mesh=split,
        in_specs=(
            P(DP, None),
            P(DP, None),
            P(DP, TENSOR),
            P(DP, TENSOR),
            P(DP, None, TENSOR),
            P(DP, TENSOR),
        ),
        out_specs=(P(DP, None), P(DP, None, TENSOR), P(DP, TENSOR)),
        check_vma=False,
    )
```

profile of v0, /device:TPU:1, one launch (start us, length us, event | category | flops | bytes accessed | tf_op | source)
XLA Modules:
  0.0 286.9 jit_solution(15581350529174634229)
XLA Ops:
  7.2 0.0 copy-start
  7.2 0.0 all-gather.5.cloned.1.call-start
  7.2 0.7 all-gather.5.cloned.1.call-update
  7.9 0.0 all-gather.7.cloned.1.call-start
  8.0 2.0 copy.20
  10.0 0.0 all-gather.7.cloned.1.call-update
  10.0 5.5 %fusion = bf16[5120,448]{0,1:T(8,128)(2,1)} fusion(bf16[256,5120]{1,0:T(8,128)(2,1)} %param.7, bf16[256,448]{0,1:T(8,128)(2,1)} %param.9, bf16[256,448]{0,1:T(8,128)(2,1)} %param.8), kind=kOutput, calls=%fused_computation.5 | convolution fusion | flops 1177616384 | bytes 7667712 | tf_op jit(solution)/shard_map/dot_general | solution.py:80
  15.5 0.0 copy-start.2
  15.5 0.0 copy-start.3
  15.5 7.7 %copy.23 = bf16[5120,448]{1,0:T(8,128)(2,1)} copy(bf16[5120,448]{0,1:T(8,128)(2,1)} %fusion) | data formatting | bytes 9175040 | tf_op jit(solution)/shard_map/dot_general | solution.py:80
  23.1 32.7 %all-gather.5.cloned.1.call-done = bf16[5120,448]{1,0:T(8,128)(2,1)} async-done(((bf16[320,448]{1,0:T(8,128)(2,1)}), bf16[5120,448]{1,0:T(8,128)(2,1)}) %all-gather.5.cloned.1.call-update) | async-done | bytes 4587536 | tf_op jit(solution)/shard_map/all_gather | solution.py:58
  55.8 0.0 copy-done.2
  55.8 0.0 copy-done.3
  55.8 5.4 %fusion.4 = (bf16[256,1,448]{0,2,1:T(8,128)(2,1)S(1)}, bf16[256,1,448]{0,2,1:T(8,128)(2,1)S(1)}) fusion(bf16[256,448]{0,1:T(8,128)(2,1)S(1)} %copy-done.2, bf16[256,448]{0,1:T(8,128)(2,1)S(1)} %copy-done.3, bf16[256,5120]{1,0:T(8,128)(2,1)} %param.7, bf16[5120,448]{1,0:T(8,128)(2,1)} %all-gather.5.cloned.1.call-done), kind=kOutput, calls=%fused_computation.16 | convolution fusion | flops 1176125440 | bytes 8126464 | tf_op jit(solution)/shard_map/dot_general | solution.py:56
  61.3 0.0 copy-done
  61.3 6.0 %convert_bitcast_fusion = bf16[5120,896]{0,1:T(8,128)(2,1)} fusion(bf16[256,896]{0,1:T(8,128)(2,1)S(1)} %bitcast.33, bf16[256,5120]{1,0:T(8,128)(2,1)S(1)} %copy-done), kind=kOutput, calls=%fused_computation.2 | convolution fusion | flops 2353397760 | bytes 12255232 | tf_op jit(solution)/shard_map/dot_general | solution.py:77
  67.3 12.9 %copy.22 = bf16[5120,896]{1,0:T(8,128)(2,1)} copy(bf16[5120,896]{0,1:T(8,128)(2,1)} %convert_bitcast_fusion) | data formatting | bytes 18350080 | tf_op jit(solution)/shard_map/dot_general | solution.py:77
  80.2 7.7 %maximum_bitcast_fusion = bf16[2,8,320,1344]{3,2,0,1:T(8,128)(2,1)S(1)} fusion(bf16[8,2,320,448]{3,2,1,0:T(8,128)(2,1)} %bitcast.29, bf16[8,2,320,896]{3,2,1,0:T(8,128)(2,1)} %bitcast.28), kind=kLoop, calls=%fused_computation | loop fusion | flops 27525120 | bytes 27525120 | tf_op jit(solution)/shard_map/transpose | solution.py:24
  87.9 3.6 %copy.24 = bf16[2,8,320,1344]{3,2,1,0:T(8,128)(2,1)S(1)} copy(bf16[2,8,320,1344]{3,2,0,1:T(8,128)(2,1)S(1)} %maximum_bitcast_fusion) | data formatting | bytes 27525120 | tf_op jit(solution)/shard_map/transpose | solution.py:24
  91.5 18.7 %all_to_all.10 = bf16[2,8,320,1344]{3,2,1,0:T(8,128)(2,1)} all-to-all(bf16[2,8,320,1344]{3,2,1,0:T(8,128)(2,1)S(1)} %copy.24), channel_id=1, replica_groups=mesh['dp_0'=2,'dp_1'=4,'dp_2'=2,'tensor_0'=4,'tensor_1'=4] {'dp_2'}, dimensions={0} | all-to-all | bytes 27525120 | tf_op jit(solution)/shard_map/all_to_all | solution.py:34
  110.2 13.1 %reduce_sum.21 = bf16[8,320,1344]{2,1,0:T(8,128)(2,1)} reduce(bf16[2,8,320,1344]{3,2,1,0:T(8,128)(2,1)} %all_to_all.10, bf16[]{:T(256)} %constant.6.clone.1), dimensions={0}, to_apply=%region_2.0 | reduce | flops 3440640 | bytes 20643842 | tf_op jit(solution)/shard_map/reduce_sum | solution.py:35
  123.3 4.8 %all-to-all-start.1 = ((bf16[8,320,1344]{2,1,0:T(8,128)(2,1)}), bf16[8,320,1344]{2,1,0:T(8,128)(2,1)}, u32[]{:S(2)}, u32[]{:S(2)}) async-start(bf16[8,320,1344]{2,1,0:T(8,128)(2,1)} %reduce_sum.21), calls=%async_computation.3 | async-start | bytes 14417920 | tf_op jit(solution)/shard_map/all_to_all | solution.py:42
  128.2 0.2 reduce-scatter.3.cloned.1.call-start
  128.4 0.0 all-gather.7.cloned.1.call-done
  128.4 11.1 %fusion.1 = bf16[256,5120]{1,0:T(8,128)(2,1)S(1)} fusion(bf16[5120,2,448]{2,0,1:T(8,128)(2,1)} %all-gather.7.cloned.1.call-done, bf16[256,1,448]{0,2,1:T(8,128)(2,1)S(1)} %get-tuple-element.4, bf16[256,1,448]{0,2,1:T(8,128)(2,1)S(1)} %get-tuple-element.3), kind=kOutput, calls=%fused_computation.6 | convolution fusion | flops 2350350336 | bytes 12255232 | tf_op jit(solution)/shard_map/dot_general | solution.py:70
  139.5 1.7 copy.21
  141.2 0.0 reduce-scatter.3.cloned.1.call-update
  141.3 0.0 reduce-scatter.5.cloned.1.call-start
  141.3 37.2 %reduce-scatter.3.cloned.1.call-done = bf16[4,16,5120]{2,1,0:T(8,128)(2,1)} async-done(((bf16[16,16,5120]{2,1,0:T(8,128)(2,1)}), bf16[4,16,5120]{2,1,0:T(8,128)(2,1)}) %reduce-scatter.3.cloned.1.call-update) | async-done | bytes 655376 | tf_op jit(solution)/shard_map/reduce_scatter | solution.py:17
  178.5 0.0 reduce-scatter.5.cloned.1.call-update
  178.5 0.0 all-gather.9.cloned.1.call-start
  178.6 34.9 %reduce-scatter.5.cloned.1.call-done = bf16[1,16,5120]{2,1,0:T(8,128)(2,1)} async-done(((bf16[4,16,5120]{2,1,0:T(8,128)(2,1)}), bf16[1,16,5120]{2,1,0:T(8,128)(2,1)}) %reduce-scatter.5.cloned.1.call-update) | async-done | bytes 163856 | tf_op jit(solution)/shard_map/reduce_scatter | solution.py:17
  213.5 0.0 all-gather.9.cloned.1.call-update
  213.5 4.7 %all-to-all-done.1 = bf16[8,320,1344]{2,1,0:T(8,128)(2,1)} async-done(((bf16[8,320,1344]{2,1,0:T(8,128)(2,1)}), bf16[8,320,1344]{2,1,0:T(8,128)(2,1)}, u32[]{:S(2)}, u32[]{:S(2)}) %all-to-all-start.1) | async-done | bytes 6881312 | tf_op jit(solution)/shard_map/all_to_all | solution.py:42
  218.2 4.3 %convert_reduce_fusion = f32[320,1344]{1,0:T(8,128)S(1)} fusion(bf16[8,320,1344]{2,1,0:T(8,128)(2,1)} %all-to-all-done.1), kind=kLoop, calls=%fused_computation.1 | loop fusion | flops 6451200 | bytes 8601600 | tf_op jit(solution)/shard_map/reduce_sum | solution.py:41
  222.5 0.0 copy-start.1
  222.5 0.1 broadcast_multiply_fusion
  222.6 1.1 slice.8
  223.7 0.9 slice.9
  224.6 3.5 %reshape.21 = f32[320,2,448]{2,1,0:T(2,128)} reshape(f32[320,896]{1,0:T(8,128)} %slice.8) | data formatting | bytes 2293760 | tf_op jit(solution)/shard_map/reshape | solution.py:89
  228.1 48.9 %all-gather.9.cloned.1.call-done = bf16[1,256,5120]{2,1,0:T(8,128)(2,1)} async-done(((bf16[1,16,5120]{2,1,0:T(8,128)(2,1)}), bf16[1,256,5120]{2,1,0:T(8,128)(2,1)}) %all-gather.9.cloned.1.call-update) | async-done | bytes 2621456 | tf_op jit(solution)/shard_map/all_gather | solution.py:76
  277.0 3.4 %copy.26 = bf16[256,5120]{1,0:T(8,128)(2,1)} copy(bf16[256,5120]{1,0:T(8,128)(2,1)} %bitcast.31) | data formatting | bytes 5242880
  280.4 0.0 copy-done.1
  (1 shorter events, 0.0 us)
Async XLA Ops:
  7.2 54.1 %copy-start = (bf16[256,5120]{1,0:T(8,128)(2,1)S(1)}, bf16[256,5120]{1,0:T(8,128)(2,1)}, u32[]{:S(2)}) copy-start(bf16[256,5120]{1,0:T(8,128)(2,1)} %param.6) | copy-start | bytes 7864324
  7.2 48.6 %all-gather.5.cloned.1.call-start = ((), (), s32[]{:S(2)}) async-start(), calls=%async_computation.4 | async-start | bytes 5570560 | tf_op jit(solution)/shard_map/all_gather | solution.py:58
  7.9 120.5 %all-gather.7.cloned.1.call-start = ((), (), s32[]{:S(2)}) async-start(), calls=%async_computation.5 | async-start | bytes 11141120 | tf_op jit(solution)/shard_map/all_gather | solution.py:68
  15.5 40.4 %copy-start.2 = (bf16[256,448]{0,1:T(8,128)(2,1)S(1)}, bf16[256,448]{0,1:T(8,128)(2,1)}, u32[]{:S(2)}) copy-start(bf16[256,448]{0,1:T(8,128)(2,1)} %param.9) | copy-start | bytes 688132
  15.5 40.4 %copy-start.3 = (bf16[256,448]{0,1:T(8,128)(2,1)S(1)}, bf16[256,448]{0,1:T(8,128)(2,1)}, u32[]{:S(2)}) copy-start(bf16[256,448]{0,1:T(8,128)(2,1)} %param.8) | copy-start | bytes 688132
  123.3 94.9 %all-to-all-start.1 = ((bf16[8,320,1344]{2,1,0:T(8,128)(2,1)}), bf16[8,320,1344]{2,1,0:T(8,128)(2,1)}, u32[]{:S(2)}, u32[]{:S(2)}) async-start(bf16[8,320,1344]{2,1,0:T(8,128)(2,1)} %reduce_sum.21), calls=%async_computation.3 | async-start | bytes 14417920 | tf_op jit(solution)/shard_map/all_to_all | solution.py:42
  128.2 50.3 %reduce-scatter.3.cloned.1.call-start = ((), (), s32[]{:S(2)}) async-start(), calls=%async_computation.6 | async-start | bytes 3276800 | tf_op jit(solution)/shard_map/reduce_scatter | solution.py:17
  141.3 72.2 %reduce-scatter.5.cloned.1.call-start = ((), (), s32[]{:S(2)}) async-start(), calls=%async_computation.7 | async-start | bytes 819200 | tf_op jit(solution)/shard_map/reduce_scatter | solution.py:17
  178.5 98.5 %all-gather.9.cloned.1.call-start = ((), (), s32[]{:S(2)}) async-start(), calls=%async_computation.8 | async-start | bytes 2785280 | tf_op jit(solution)/shard_map/all_gather | solution.py:76
  222.5 57.9 %copy-start.1 = (bf16[256,5120]{1,0:T(8,128)(2,1)S(1)}, bf16[256,5120]{1,0:T(8,128)(2,1)}, u32[]{:S(2)}) copy-start(bf16[256,5120]{1,0:T(8,128)(2,1)} %param.6) | copy-start | bytes 7864324
Sparse Core Ops, SparseCore 0:
  9.8 45.9 all-gather.4
  58.2 64.2 all-gather.6
  141.4 37.0 reduce-scatter.2
  180.9 32.5 reduce-scatter.4
  215.8 61.1 all-gather.8
where the time goes:
time: 288 us; the launch traced here: 287 us
  waiting for transfers between devices  159 us (55%)
  local copies, waits for them, and re-layouts  36.8 us (13%)
  matrix products  28 us (10%)
  other arithmetic  25.3 us (9%)
  blocking collectives  18.7 us (6%)
  between operations  13.9 us (5%)
  starting transfers between devices  5.22 us (2%)
    reduce_scatter x2, waiting for transfers between devices, sum_in_order(): pieces = lax.psum_scatter(pieces, axes[k], scatter_dimension=0, tiled=True)  72.1 us
    all_gather x1, waiting for transfers between devices, per_device(): lax.all_gather(share_block.astype(jnp.bfloat16), TENSOR, axis=0, tiled=True)  48.9 us
    all_gather x1, waiting for transfers between devices, per_device(): lax.all_gather(down_weight, DP, axis=0, tiled=True)  32.7 us
    all_to_all x1, blocking collectives, sum_at_owner(): pieces = lax.all_to_all(split_up(x, dim, devices), axis, 0, 0, tiled=True)  18.7 us
    reduce_sum x1, other arithmetic, sum_at_owner(): return jnp.sum(pieces.astype(jnp.float32), axis=0)  13.1 us
    dot_general x1, local copies, waits for them, and re-layouts, per_device(): lax.dot_general(activations, grad_hidden, (((0,), (0,)), ((), ())), prefe...  12.9 us
    dot_general x1, matrix products, per_device(): lax.dot_general(grad_hidden, flattened, (((1,), (1,)), ((), ())), preferr...  11.1 us
    transpose x1, other arithmetic, split_up(): return jnp.moveaxis(pieces, dim, 0)  7.67 us
  transfers between devices with their start and end apart: 6, of which 5 were waited for; matrix products, arithmetic and copies ran while one was open for 30% of the time, Pallas kernels for 0%

commit v1 on v0

--- a/solution.py
+++ b/solution.py
@@ -73,7 +73,11 @@
     share_block = sum_by_axis(partial_sum.astype(jnp.bfloat16), TENSOR, (1, 0), 0).astype(
         jnp.float32
     )
-    grad_input = lax.all_gather(share_block.astype(jnp.bfloat16), TENSOR, axis=0, tiled=True)
+    block = share_block.astype(jnp.bfloat16)
+    size = lax.axis_size(TENSOR)
+    parts = jnp.stack([block for _ in range(size)])
+    parts = lax.all_to_all(parts, TENSOR, split_axis=0, concat_axis=0)
+    grad_input = jnp.concatenate(parts, axis=0)
     gate_part = lax.dot_general(
         activations, grad_hidden, (((0,), (0,)), ((), ())), preferred_element_type=jnp.float32
     )

time: 288 us -> 306 us (1.062)
  starting transfers between devices: 5.22 us -> 13.8 us
  waiting for transfers between devices: 159 us -> 164 us
    all_to_all x0 -> x1, waiting for transfers between devices: none -> 54.2 us  [per_device(): parts = lax.all_to_all(parts, TENSOR, split_axis=0, concat_axis=0)]
    all_gather x1 -> x0, waiting for transfers between devices: 48.9 us -> none  [per_device(): lax.all_gather(share_block.astype(jnp.bfloat16), TENSOR, axis=0, tiled=True)]
    all_to_all x1, waiting for transfers between devices: 4.67 us -> 39.7 us  [sum_in_two_steps(): lax.all_to_all(own.astype(jnp.bfloat16), far, 0, 0, tiled=True)]
    reduce_scatter x2, waiting for transfers between devices: 72.1 us -> 37.2 us  [sum_in_order(): pieces = lax.psum_scatter(pieces, axes[k], scatter_dimension=0, tiled=True)]
    all_to_all x0 -> x1, starting transfers between devices: none -> 8.63 us  [per_device(): parts = lax.all_to_all(parts, TENSOR, split_axis=0, concat_axis=0)]
    another operation x0 -> x2, local copies, waits for them, and re-layouts: none -> 4.43 us  [the longest x1 2.7 us: per_device(): parts = jnp.stack([block for _ in range(size)])]
  transfers between devices with their start and end apart: 6 -> 6, of which waited for: 5 -> 4; matrix products, arithmetic and copies ran while one was open for 30% -> 29% of each run, Pallas kernels for 0% -> 0%
where the time goes in v1:
time: 306 us; the launch traced here: 304 us
  waiting for transfers between devices  164 us (54%)
  local copies, waits for them, and re-layouts  39.6 us (13%)
  matrix products  28 us (9%)
  other arithmetic  25.3 us (8%)
  blocking collectives  18.7 us (6%)
  between operations  13.9 us (5%)
  starting transfers between devices  13.8 us (5%)
    all_to_all x1, waiting for transfers between devices, per_device(): parts = lax.all_to_all(parts, TENSOR, split_axis=0, concat_axis=0)  54.2 us
    all_to_all x1, waiting for transfers between devices, sum_in_two_steps(): lax.all_to_all(own.astype(jnp.bfloat16), far, 0, 0, tiled=True)  39.7 us
    reduce_scatter x2, waiting for transfers between devices, sum_in_order(): pieces = lax.psum_scatter(pieces, axes[k], scatter_dimension=0, tiled=True)  37.2 us
    all_gather x1, waiting for transfers between devices, per_device(): lax.all_gather(down_weight, DP, axis=0, tiled=True)  32.6 us
    all_to_all x1, blocking collectives, sum_at_owner(): pieces = lax.all_to_all(split_up(x, dim, devices), axis, 0, 0, tiled=True)  18.7 us
    reduce_sum x1, other arithmetic, sum_at_owner(): return jnp.sum(pieces.astype(jnp.float32), axis=0)  13.1 us
    dot_general x1, local copies, waits for them, and re-layouts, per_device(): lax.dot_general(activations, grad_hidden, (((0,), (0,)), ((), ())), prefe...  12.8 us
    dot_general x1, matrix products, per_device(): lax.dot_general(grad_hidden, flattened, (((1,), (1,)), ((), ())), preferr...  11.1 us
  transfers between devices with their start and end apart: 6, of which 4 were waited for; matrix products, arithmetic and copies ran while one was open for 29% of the time, Pallas kernels for 0%

profile of v1, /device:TPU:1, one launch (start us, length us, event | category | flops | bytes accessed | tf_op | source)
XLA Modules:
  0.0 303.6 jit_solution(14931602729919223324)
XLA Ops:
  7.2 0.0 copy-start
  7.2 0.0 all-gather.3.cloned.1.call-start
  7.2 0.7 all-gather.3.cloned.1.call-update
  7.9 0.0 all-gather.5.cloned.1.call-start
  8.0 2.0 copy.19
  10.0 0.0 all-gather.5.cloned.1.call-update
  10.0 5.5 %fusion = bf16[5120,448]{0,1:T(8,128)(2,1)} fusion(bf16[256,5120]{1,0:T(8,128)(2,1)} %param.7, bf16[256,448]{0,1:T(8,128)(2,1)} %param.9, bf16[256,448]{0,1:T(8,128)(2,1)} %param.8), kind=kOutput, calls=%fused_computation.5 | convolution fusion | flops 1177616384 | bytes 7667712 | tf_op jit(solution)/shard_map/dot_general | solution.py:84
  15.5 0.0 copy-start.2
  15.5 0.0 copy-start.3
  15.5 7.7 %copy.22 = bf16[5120,448]{1,0:T(8,128)(2,1)} copy(bf16[5120,448]{0,1:T(8,128)(2,1)} %fusion) | data formatting | bytes 9175040 | tf_op jit(solution)/shard_map/dot_general | solution.py:84
  23.2 32.6 %all-gather.3.cloned.1.call-done = bf16[5120,448]{1,0:T(8,128)(2,1)} async-done(((bf16[320,448]{1,0:T(8,128)(2,1)}), bf16[5120,448]{1,0:T(8,128)(2,1)}) %all-gather.3.cloned.1.call-update) | async-done | bytes 4587536 | tf_op jit(solution)/shard_map/all_gather | solution.py:58
  55.8 0.0 copy-done.2
  55.8 0.0 copy-done.3
  55.8 5.4 %fusion.4 = (bf16[256,1,448]{0,2,1:T(8,128)(2,1)S(1)}, bf16[256,1,448]{0,2,1:T(8,128)(2,1)S(1)}) fusion(bf16[256,448]{0,1:T(8,128)(2,1)S(1)} %copy-done.2, bf16[256,448]{0,1:T(8,128)(2,1)S(1)} %copy-done.3, bf16[256,5120]{1,0:T(8,128)(2,1)} %param.7, bf16[5120,448]{1,0:T(8,128)(2,1)} %all-gather.3.cloned.1.call-done), kind=kOutput, calls=%fused_computation.16 | convolution fusion | flops 1176125440 | bytes 8126464 | tf_op jit(solution)/shard_map/dot_general | solution.py:56
  61.3 0.0 copy-done
  61.3 6.0 %convert_bitcast_fusion = bf16[5120,896]{0,1:T(8,128)(2,1)} fusion(bf16[256,896]{0,1:T(8,128)(2,1)S(1)} %bitcast.33, bf16[256,5120]{1,0:T(8,128)(2,1)S(1)} %copy-done), kind=kOutput, calls=%fused_computation.2 | convolution fusion | flops 2353397760 | bytes 12255232 | tf_op jit(solution)/shard_map/dot_general | solution.py:81
  67.3 12.8 %copy.21 = bf16[5120,896]{1,0:T(8,128)(2,1)} copy(bf16[5120,896]{0,1:T(8,128)(2,1)} %convert_bitcast_fusion) | data formatting | bytes 18350080 | tf_op jit(solution)/shard_map/dot_general | solution.py:81
  80.1 7.7 %maximum_bitcast_fusion = bf16[2,8,320,1344]{3,2,0,1:T(8,128)(2,1)S(1)} fusion(bf16[8,2,320,448]{3,2,1,0:T(8,128)(2,1)} %bitcast.30, bf16[8,2,320,896]{3,2,1,0:T(8,128)(2,1)} %bitcast.29), kind=kLoop, calls=%fused_computation | loop fusion | flops 27525120 | bytes 27525120 | tf_op jit(solution)/shard_map/transpose | solution.py:24
  87.8 3.6 %copy.23 = bf16[2,8,320,1344]{3,2,1,0:T(8,128)(2,1)S(1)} copy(bf16[2,8,320,1344]{3,2,0,1:T(8,128)(2,1)S(1)} %maximum_bitcast_fusion) | data formatting | bytes 27525120 | tf_op jit(solution)/shard_map/transpose | solution.py:24
  91.5 18.7 %all_to_all.15 = bf16[2,8,320,1344]{3,2,1,0:T(8,128)(2,1)} all-to-all(bf16[2,8,320,1344]{3,2,1,0:T(8,128)(2,1)S(1)} %copy.23), channel_id=1, replica_groups=mesh['dp_0'=2,'dp_1'=4,'dp_2'=2,'tensor_0'=4,'tensor_1'=4] {'dp_2'}, dimensions={0} | all-to-all | bytes 27525120 | tf_op jit(solution)/shard_map/all_to_all | solution.py:34
  110.2 13.1 %reduce_sum.21 = bf16[8,320,1344]{2,1,0:T(8,128)(2,1)} reduce(bf16[2,8,320,1344]{3,2,1,0:T(8,128)(2,1)} %all_to_all.15, bf16[]{:T(256)} %constant.6.clone.1), dimensions={0}, to_apply=%region_2.0 | reduce | flops 3440640 | bytes 20643842 | tf_op jit(solution)/shard_map/reduce_sum | solution.py:35
  123.3 4.8 %all-to-all-start.2 = ((bf16[8,320,1344]{2,1,0:T(8,128)(2,1)}), bf16[8,320,1344]{2,1,0:T(8,128)(2,1)}, u32[]{:S(2)}, u32[]{:S(2)}) async-start(bf16[8,320,1344]{2,1,0:T(8,128)(2,1)} %reduce_sum.21), calls=%async_computation.4 | async-start | bytes 14417920 | tf_op jit(solution)/shard_map/all_to_all | solution.py:42
  128.2 0.2 reduce-scatter.3.cloned.1.call-start
  128.4 0.0 all-gather.5.cloned.1.call-done
  128.4 11.1 %fusion.1 = bf16[256,5120]{1,0:T(8,128)(2,1)S(1)} fusion(bf16[5120,2,448]{2,0,1:T(8,128)(2,1)} %all-gather.5.cloned.1.call-done, bf16[256,1,448]{0,2,1:T(8,128)(2,1)S(1)} %get-tuple-element.4, bf16[256,1,448]{0,2,1:T(8,128)(2,1)S(1)} %get-tuple-element.3), kind=kOutput, calls=%fused_computation.6 | convolution fusion | flops 2350350336 | bytes 12255232 | tf_op jit(solution)/shard_map/dot_general | solution.py:70
  139.5 1.7 copy.20
  141.2 0.0 reduce-scatter.3.cloned.1.call-update
  141.3 0.0 reduce-scatter.5.cloned.1.call-start
  141.3 37.2 %reduce-scatter.3.cloned.1.call-done = bf16[4,16,5120]{2,1,0:T(8,128)(2,1)} async-done(((bf16[16,16,5120]{2,1,0:T(8,128)(2,1)}), bf16[4,16,5120]{2,1,0:T(8,128)(2,1)}) %reduce-scatter.3.cloned.1.call-update) | async-done | bytes 655376 | tf_op jit(solution)/shard_map/reduce_scatter | solution.py:17
  178.5 0.0 reduce-scatter.5.cloned.1.call-update
  178.5 39.7 %all-to-all-done.2 = bf16[8,320,1344]{2,1,0:T(8,128)(2,1)} async-done(((bf16[8,320,1344]{2,1,0:T(8,128)(2,1)}), bf16[8,320,1344]{2,1,0:T(8,128)(2,1)}, u32[]{:S(2)}, u32[]{:S(2)}) %all-to-all-start.2) | async-done | bytes 6881312 | tf_op jit(solution)/shard_map/all_to_all | solution.py:42
  218.2 0.0 reduce-scatter.5.cloned.1.call-done
  218.2 2.7 stack.14
  220.9 8.6 %all-to-all-start = ((bf16[16,16,5120]{2,1,0:T(8,128)(2,1)}), bf16[16,16,5120]{2,1,0:T(8,128)(2,1)}, u32[]{:S(2)}, u32[]{:S(2)}) async-start(bf16[16,16,5120]{2,1,0:T(8,128)(2,1)} %stack.14), calls=%async_computation.2 | async-start | bytes 5242880 | tf_op jit(solution)/shard_map/all_to_all | solution.py:79
  229.5 4.3 %convert_reduce_fusion = f32[320,1344]{1,0:T(8,128)S(1)} fusion(bf16[8,320,1344]{2,1,0:T(8,128)(2,1)} %all-to-all-done.2), kind=kLoop, calls=%fused_computation.1 | loop fusion | flops 6451200 | bytes 8601600 | tf_op jit(solution)/shard_map/reduce_sum | solution.py:41
  233.8 0.0 copy-start.1
  233.8 0.1 broadcast_multiply_fusion
  234.0 1.1 slice.8
  235.0 0.9 slice.9
  236.0 3.5 %reshape.27 = f32[320,2,448]{2,1,0:T(2,128)} reshape(f32[320,896]{1,0:T(8,128)} %slice.8) | data formatting | bytes 2293760 | tf_op jit(solution)/shard_map/reshape | solution.py:93
  239.5 54.2 %all-to-all-done = bf16[16,16,5120]{2,1,0:T(8,128)(2,1)} async-done(((bf16[16,16,5120]{2,1,0:T(8,128)(2,1)}), bf16[16,16,5120]{2,1,0:T(8,128)(2,1)}, u32[]{:S(2)}, u32[]{:S(2)}) %all-to-all-start) | async-done | bytes 2621472 | tf_op jit(solution)/shard_map/all_to_all | solution.py:79
  293.6 3.4 %copy.25 = bf16[256,5120]{1,0:T(8,128)(2,1)} copy(bf16[256,5120]{1,0:T(8,128)(2,1)} %bitcast.7) | data formatting | bytes 5242880
  297.0 0.0 copy-done.1
  (1 shorter events, 0.0 us)
Async XLA Ops:
  7.2 54.1 %copy-start = (bf16[256,5120]{1,0:T(8,128)(2,1)S(1)}, bf16[256,5120]{1,0:T(8,128)(2,1)}, u32[]{:S(2)}) copy-start(bf16[256,5120]{1,0:T(8,128)(2,1)} %param.6) | copy-start | bytes 7864324
  7.2 48.6 %all-gather.3.cloned.1.call-start = ((), (), s32[]{:S(2)}) async-start(), calls=%async_computation.5 | async-start | bytes 5570560 | tf_op jit(solution)/shard_map/all_gather | solution.py:58
  7.9 120.5 %all-gather.5.cloned.1.call-start = ((), (), s32[]{:S(2)}) async-start(), calls=%async_computation.6 | async-start | bytes 11141120 | tf_op jit(solution)/shard_map/all_gather | solution.py:68
  15.5 40.4 %copy-start.2 = (bf16[256,448]{0,1:T(8,128)(2,1)S(1)}, bf16[256,448]{0,1:T(8,128)(2,1)}, u32[]{:S(2)}) copy-start(bf16[256,448]{0,1:T(8,128)(2,1)} %param.9) | copy-start | bytes 688132
  15.5 40.4 %copy-start.3 = (bf16[256,448]{0,1:T(8,128)(2,1)S(1)}, bf16[256,448]{0,1:T(8,128)(2,1)}, u32[]{:S(2)}) copy-start(bf16[256,448]{0,1:T(8,128)(2,1)} %param.8) | copy-start | bytes 688132
  123.3 94.9 %all-to-all-start.2 = ((bf16[8,320,1344]{2,1,0:T(8,128)(2,1)}), bf16[8,320,1344]{2,1,0:T(8,128)(2,1)}, u32[]{:S(2)}, u32[]{:S(2)}) async-start(bf16[8,320,1344]{2,1,0:T(8,128)(2,1)} %reduce_sum.21), calls=%async_computation.4 | async-start | bytes 14417920 | tf_op jit(solution)/shard_map/all_to_all | solution.py:42
  128.2 50.3 %reduce-scatter.3.cloned.1.call-start = ((), (), s32[]{:S(2)}) async-start(), calls=%async_computation.7 | async-start | bytes 3276800 | tf_op jit(solution)/shard_map/reduce_scatter | solution.py:17
  141.3 76.9 %reduce-scatter.5.cloned.1.call-start = ((), (), s32[]{:S(2)}) async-start(), calls=%async_computation.8 | async-start | bytes 819200 | tf_op jit(solution)/shard_map/reduce_scatter | solution.py:17
  220.9 72.8 %all-to-all-start = ((bf16[16,16,5120]{2,1,0:T(8,128)(2,1)}), bf16[16,16,5120]{2,1,0:T(8,128)(2,1)}, u32[]{:S(2)}, u32[]{:S(2)}) async-start(bf16[16,16,5120]{2,1,0:T(8,128)(2,1)} %stack.14), calls=%async_computation.2 | async-start | bytes 5242880 | tf_op jit(solution)/shard_map/all_to_all | solution.py:79
  233.8 63.2 %copy-start.1 = (bf16[256,5120]{1,0:T(8,128)(2,1)S(1)}, bf16[256,5120]{1,0:T(8,128)(2,1)}, u32[]{:S(2)}) copy-start(bf16[256,5120]{1,0:T(8,128)(2,1)} %param.6) | copy-start | bytes 7864324
Sparse Core Ops, SparseCore 0:
  9.8 45.9 all-gather.2
  58.2 64.2 all-gather.4
  141.4 37.0 reduce-scatter.2
  180.9 32.5 reduce-scatter.4
